TPU v7x, 1024 devices: a whole 8x8x8 slice. The times are simulated.
1024 devices in a mesh: dp: 16 (over x_lo, z), expert: 64 (over x_hi, y, core).
Axes of the slice: x: 8 (x_hi: 4, x_lo: 2; x = x_hi * 2 + x_lo), y: 8, z: 8, core: 2. Of those that a mesh axis runs over, the one named last changes fastest.
Arguments:
- tokens: bfloat16 [8192, 4096], P('expert', 'dp'), may hold values from -6 to 6
- grad_out: bfloat16 [8192, 4096], P('expert', 'dp'), may hold values from -6 to 6
- expert_ids: int32 [8192, 2], P('expert'), may hold values from 0 to 63, all different within a row; in each aligned block of 128 rows (0 to 127, 128 to 255, ...) at most 6 rows name the same one
- route_weights: float32 [8192, 2], P('expert'), may hold values from 0.05 to 1
- gate_weight: bfloat16 [64, 4096, 768], P('expert', 'dp'), may hold values from -0.09375 to 0.09375
- up_weight: bfloat16 [64, 4096, 768], P('expert', 'dp'), may hold values from -0.09375 to 0.09375
- down_weight: bfloat16 [64, 768, 4096], P('expert', None, 'dp'), may hold values from -0.21875 to 0.21875
Outputs:
- mixed: bfloat16 [8192, 4096], P('expert', 'dp')
- grad_tokens: bfloat16 [8192, 4096], P('expert', 'dp')
- grad_route: float32 [8192, 2], P('expert')
- grad_gate: bfloat16 [64, 4096, 768], P('expert', 'dp')
- grad_up: bfloat16 [64, 4096, 768], P('expert', 'dp')
- grad_down: bfloat16 [64, 768, 4096], P('expert', None, 'dp')
Inputs may be any that keep to these rules, and one draw needn't show every extreme that they name: `expert_ids`: each token names 2 different experts; in each aligned block of 128 tokens (the tokens held by each position along `expert`) no expert is named by more than 6 tokens, a bound that some block reaches.
All inputs are finite; a program needn't handle non-finite values.
Results may differ from a plain program's by a relative error of at most 0.029.
Values may be sent and summed in bfloat16 or wider, within the bound.
A program may use at most 32 MiB of HBM per device.

v0:
```python
import jax
import jax.numpy as jnp
from jax import lax
from jax.sharding import PartitionSpec as P


def in_one_piece(arrays, axis, split_dim, concat_dim, along):
    ends, at = ([], 0)
    for a in arrays[:-1]:
        at += a.shape[along]
        ends.append(at)
    both = jnp.concatenate(arrays, axis=along)
    return tuple(
        jnp.split(
            lax.all_to_all(both, axis, split_axis=split_dim, concat_axis=concat_dim, tiled=True),
            ends,
            axis=along,
        )
    )


def split_up(shard, dim, devices):
    before, after = (shard.shape[:dim], shard.shape[dim + 1 :])
    return jnp.moveaxis(shard.reshape(*before, devices, -1, *after), dim, 0)


def summed_on_arrival(shard, axis, dim):
    devices = lax.axis_size(axis)
    pieces = lax.all_to_all(split_up(shard, dim, devices), axis, 0, 0, tiled=True)
    return jnp.sum(pieces.astype(jnp.float32), axis=0)


def in_one_piece_2(arrays, axis, dim, along):
    ends, at = ([], 0)
    for a in arrays[:-1]:
        at += a.shape[along]
        ends.append(at)
    both = jnp.concatenate(arrays, axis=along)
    return tuple(jnp.split(summed_on_arrival(both, axis, dim), ends, axis=along))


def gather_turned(arrays, axis, dims):
    turned = [jnp.moveaxis(a, dim, 0) for a, dim in zip(arrays, dims)]
    widths = [t[0].size for t in turned]
    both = jnp.concatenate([t.reshape(-1, w) for t, w in zip(turned, widths)], axis=1)
    result = lax.all_gather(both, axis, axis=0, tiled=True)
    pieces = jnp.split(result, [sum(widths[:k]) for k in range(1, len(widths))], axis=1)
    return tuple(
        (
            jnp.moveaxis(b.reshape(-1, *t.shape[1:]), 0, dim)
            for b, t, dim in zip(pieces, turned, dims)
        )
    )


def from_everyone(shard, axis):
    devices = lax.axis_size(axis)
    return lax.all_to_all(
        jnp.broadcast_to(shard[None], (devices, *shard.shape)), axis, 0, 0, tiled=True
    )


def over_copies(shard, axis):
    return from_everyone(shard, axis).sum(axis=0)


def activate(gate_sum, up_sum, back_sum):
    gate_sigmoid = jax.nn.sigmoid(gate_sum)
    swished = gate_sum * gate_sigmoid
    hidden = (swished * up_sum).astype(jnp.bfloat16)
    gate_grad = (back_sum * up_sum * gate_sigmoid * (1.0 + gate_sum * (1.0 - gate_sigmoid))).astype(
        jnp.bfloat16
    )
    up_grad = (back_sum * swished).astype(jnp.bfloat16)
    return (hidden, gate_grad, up_grad)


def to_sources(expert_rows, expert_count):
    local_count, row_count, feature_share = expert_rows.shape
    capacity = row_count // expert_count
    ordered = expert_rows.reshape(local_count, expert_count, capacity, feature_share).transpose(
        1, 0, 2, 3
    )
    return ordered.reshape(expert_count * local_count * capacity, feature_share)


def from_sources(arrived, expert_count, local_count):
    capacity = arrived.shape[0] // (expert_count * local_count)
    feature_share = arrived.shape[1]
    ordered = arrived.reshape(expert_count, local_count, capacity, feature_share).transpose(
        1, 0, 2, 3
    )
    return ordered.reshape(local_count, expert_count * capacity, feature_share)


def local(tokens, grad_out, expert_ids, route_weights, gate_weight, up_weight, down_weight):
    expert_count = lax.axis_size("expert")
    local_count = gate_weight.shape[0]
    experts = local_count * expert_count
    tok_rows, feature_share = tokens.shape
    top_count = expert_ids.shape[1]
    capacity = max(2, 3 * tok_rows * top_count // (2 * experts))
    flat_ids = expert_ids.reshape(-1)
    assigned = flat_ids.shape[0]
    onehot = (flat_ids[:, None] == jnp.arange(experts, dtype=jnp.int32)[None, :]).astype(jnp.int32)
    before = jnp.cumsum(onehot, axis=0) - onehot
    position = jnp.sum(before * onehot, axis=1)
    slot_index = flat_ids * capacity + position
    owners = (
        jnp.zeros((experts * capacity,), jnp.int32)
        .at[slot_index]
        .set(jnp.arange(assigned, dtype=jnp.int32) + 1)
    )
    filled = owners > 0
    source = jnp.maximum(owners - 1, 0)
    token_index = source // top_count
    send_rows = jnp.where(filled[:, None], tokens[token_index], jnp.zeros((), jnp.bfloat16))
    scaled = route_weights.reshape(-1)[source][:, None] * grad_out[token_index].astype(jnp.float32)
    send_grads = jnp.where(filled[:, None], scaled, 0.0).astype(jnp.bfloat16)
    arrived_rows, arrived_grads = in_one_piece((send_rows, send_grads), "expert", 0, 0, 1)
    expert_rows = from_sources(arrived_rows, expert_count, local_count)
    expert_grads = from_sources(arrived_grads, expert_count, local_count)
    gate_part = jnp.einsum(
        "erd,edh->erh", expert_rows, gate_weight, preferred_element_type=jnp.float32
    )
    up_part = jnp.einsum("erd,edh->erh", expert_rows, up_weight, preferred_element_type=jnp.float32)
    back_part = jnp.einsum(
        "erd,ehd->erh", expert_grads, down_weight, preferred_element_type=jnp.float32
    )
    summed = in_one_piece_2(
        (
            gate_part.astype(jnp.bfloat16),
            up_part.astype(jnp.bfloat16),
            back_part.astype(jnp.bfloat16),
        ),
        "dp",
        2,
        0,
    )
    pieces = activate(summed[0], summed[1], summed[2])
    hidden, gate_grad, up_grad = gather_turned((pieces[0], pieces[1], pieces[2]), "dp", (2, 2, 2))
    out_rows = jnp.einsum(
        "erh,ehd->erd", hidden, down_weight, preferred_element_type=jnp.float32
    ).astype(jnp.bfloat16)
    grad_down = jnp.einsum(
        "erh,erd->ehd", hidden, expert_grads, preferred_element_type=jnp.float32
    ).astype(jnp.bfloat16)
    grad_gate = jnp.einsum(
        "erd,erh->edh", expert_rows, gate_grad, preferred_element_type=jnp.float32
    ).astype(jnp.bfloat16)
    grad_up = jnp.einsum(
        "erd,erh->edh", expert_rows, up_grad, preferred_element_type=jnp.float32
    ).astype(jnp.bfloat16)
    input_rows = (
        jnp.einsum("erh,edh->erd", gate_grad, gate_weight, preferred_element_type=jnp.float32)
        + jnp.einsum("erh,edh->erd", up_grad, up_weight, preferred_element_type=jnp.float32)
    ).astype(jnp.bfloat16)
    out_back, input_back = in_one_piece(
        (to_sources(out_rows, expert_count), to_sources(input_rows, expert_count)),
        "expert",
        0,
        0,
        1,
    )
    out_assign = (
        out_back[slot_index].reshape(tok_rows, top_count, feature_share).astype(jnp.float32)
    )
    input_assign = (
        input_back[slot_index].reshape(tok_rows, top_count, feature_share).astype(jnp.float32)
    )
    mixed = jnp.einsum("tk,tkd->td", route_weights, out_assign).astype(jnp.bfloat16)
    grad_tokens = jnp.sum(input_assign, axis=1).astype(jnp.bfloat16)
    partial_dots = jnp.einsum("td,tkd->tk", grad_out.astype(jnp.float32), out_assign)
    grad_route = over_copies(partial_dots, "dp")
    return (mixed, grad_tokens, grad_route, grad_gate, grad_up, grad_down)


def solution(mesh):
    placed = (
        P("expert", "dp"),
        P("expert", "dp"),
        P("expert", None),
        P("expert", None),
        P("expert", "dp", None),
        P("expert", "dp", None),
        P("expert", None, "dp"),
    )
    return jax.shard_map(
        local,
        mesh=mesh,
        in_specs=placed,
        out_specs=(
            P("expert", "dp"),
            P("expert", "dp"),
            P("expert", None),
            P("expert", "dp", None),
            P("expert", "dp", None),
            P("expert", None, "dp"),
        ),
        check_vma=False,
    )
```

profile of v0, /device:TPU:1, one launch (start us, length us, event | category | flops | bytes accessed | tf_op | source)
XLA Modules:
  0.0 245.7 jit_solution(13445789879733265661)
XLA Ops:
  7.2 0.8 copy.22
  8.1 0.1 eq.29
  8.2 0.1 eq.25
  8.4 0.7 broadcast_multiply_fusion
  9.1 0.6 reduce-window.6
  9.7 0.2 slice_reduce_fusion
  9.9 0.1 copy.21
  10.0 0.1 mul.53
  10.2 0.1 fusion.22
  10.3 1.4 scatter_custom_fusion
  11.7 2.1 gather_fusion.2
  13.8 0.1 reshape.195
  13.9 0.1 copy.25
  14.0 0.1 reshape.180
  14.1 2.8 %gather_fusion.1 = f32[384]{0:T(512)S(1)} fusion(f32[256]{0:T(256)S(1)} %reshape.180, s32[1024]{0:T(1024)S(1)} %get-tuple-element.13), kind=kCustom, calls=%fused_computation.1 | custom fusion | bytes 4608 | tf_op jit(solution)/shard_map/gather | solution.py:118
  16.9 0.1 mul.55
  17.1 0.2 broadcast_in_dim.44
  17.3 2.1 gather_fusion
  19.3 0.1 gather.18
  19.4 0.1 broadcast_select_fusion
  19.5 0.2 select_convert_fusion
  19.7 0.1 pad_maximum_fusion
  19.8 35.6 %all_to_all.28 = bf16[64,6,512]{2,1,0:T(8,128)(2,1)S(1)} all-to-all(bf16[64,6,512]{2,1,0:T(8,128)(2,1)S(1)} %pad_maximum_fusion), channel_id=1, replica_groups=mesh['dp'=16,'expert'=64] {'expert'}, dimensions={0} | all-to-all | bytes 786432 | tf_op jit(solution)/shard_map/all_to_all | solution.py:15
  55.4 0.1 all_to_all.19
  55.6 0.3 convolution_convert_fusion.2
  55.9 0.3 copy.26
  56.2 0.2 copy-done.4
  56.4 0.3 convolution_convert_fusion.1
  56.8 0.3 copy.27
  57.1 1.3 convolution_convert_fusion
  58.4 0.3 copy.28
  58.7 0.2 maximum_bitcast_fusion
  59.0 0.2 copy.29
  59.2 55.9 %all_to_all.29 = bf16[16,3,384,48]{2,3,1,0:T(8,128)(2,1)S(1)} all-to-all(bf16[16,3,384,48]{2,3,1,0:T(8,128)(2,1)S(1)} %copy.29), channel_id=1, replica_groups=mesh['dp'=16,'expert'=64] {'dp'}, dimensions={0} | all-to-all | bytes 3538944 | tf_op jit(solution)/shard_map/all_to_all | solution.py:29
  115.0 0.3 convert_reduce_fusion
  115.3 0.1 fusion.24
  115.3 0.7 pad_maximum_fusion.2
  116.0 62.2 %all-gather.2.cloned.1.call-done = bf16[768,1152]{1,0:T(8,128)(2,1)} async-done(((bf16[48,1152]{1,0:T(8,128)(2,1)}), bf16[768,1152]{1,0:T(8,128)(2,1)}) %all-gather.2.cloned.1.call-update) | async-done | bytes 1769488 | tf_op jit(solution)/shard_map/all_gather | solution.py:46
  178.2 1.6 fusion.4
  179.7 1.4 fusion.3
  181.2 0.1 concatenate.32
  181.3 1.4 convolution_convert_fusion.6
  182.6 0.1 concatenate.31
  182.7 0.9 pad_maximum_fusion.1
  183.6 22.3 %all-to-all-start.2 = ((bf16[64,6,512]{2,1,0:T(8,128)(2,1)}), bf16[64,6,512]{2,1,0:T(8,128)(2,1)S(1)}, u32[]{:S(2)}, u32[]{:S(2)}) async-start(bf16[64,6,512]{2,1,0:T(8,128)(2,1)} %pad_maximum_fusion.1), calls=%async_computation.2 | async-start | bytes 1048576 | tf_op jit(solution)/shard_map/all_to_all | solution.py:15
  205.9 0.8 copy.31
  206.7 1.1 fusion
  207.8 1.1 fusion.1
  209.0 1.1 fusion.2
  210.1 14.6 %all-to-all-done.2 = bf16[64,6,512]{2,1,0:T(8,128)(2,1)S(1)} async-done(((bf16[64,6,512]{2,1,0:T(8,128)(2,1)}), bf16[64,6,512]{2,1,0:T(8,128)(2,1)S(1)}, u32[]{:S(2)}, u32[]{:S(2)}) %all-to-all-start.2) | async-done | bytes 393248 | tf_op jit(solution)/shard_map/all_to_all | solution.py:15
  224.8 0.1 all_to_all.22
  224.9 1.2 gather_fusion.3
  226.1 0.1 reshape.193
  226.2 0.3 fusion.13
  226.4 0.1 copy.34
  226.5 0.6 broadcast_in_dim.50
  227.1 3.8 %all-to-all-start.3 = ((f32[16,128,2]{1,2,0:T(2,128)}), f32[16,128,2]{1,2,0:T(2,128)S(1)}, u32[]{:S(2)}, u32[]{:S(2)}) async-start(f32[16,128,2]{1,2,0:T(2,128)} %broadcast_in_dim.50), calls=%async_computation.3 | async-start | bytes 32768 | tf_op jit(solution)/shard_map/all_to_all | solution.py:58
  231.0 0.3 fusion.31
  231.3 1.2 gather_fusion.4
  232.4 0.1 reshape.194
  232.5 0.6 copy.44
  233.1 0.9 reduce_sum.44
  234.1 4.2 %all-to-all-done.3 = f32[16,128,2]{1,2,0:T(2,128)S(1)} async-done(((f32[16,128,2]{1,2,0:T(2,128)}), f32[16,128,2]{1,2,0:T(2,128)S(1)}, u32[]{:S(2)}, u32[]{:S(2)}) %all-to-all-start.3) | async-done | bytes 16416 | tf_op jit(solution)/shard_map/all_to_all | solution.py:58
  238.3 0.6 reduce_sum.45
  (27 shorter events, 0.2 us)
Async XLA Ops:
  7.2 48.4 %copy-start = (bf16[1,256,768]{2,1,0:T(8,128)(2,1)S(1)}, bf16[1,256,768]{2,1,0:T(8,128)(2,1)}, u32[]{:S(2)}) copy-start(bf16[1,256,768]{2,1,0:T(8,128)(2,1)} %param.11) | copy-start | bytes 1179652
  7.2 4.5 %copy-start.2 = (bf16[128,256]{1,0:T(8,128)(2,1)S(1)}, bf16[128,256]{1,0:T(8,128)(2,1)}, u32[]{:S(2)}) copy-start(bf16[128,256]{1,0:T(8,128)(2,1)} %param.8) | copy-start | bytes 196612
  7.2 6.7 %copy-start.7 = (f32[128,2]{0,1:T(2,128)S(1)}, f32[128,2]{0,1:T(2,128)}, u32[]{:S(2)}) copy-start(f32[128,2]{0,1:T(2,128)} %param.10) | copy-start | bytes 3076
  7.2 171.0 %all-gather.2.cloned.1.call-start = ((), (), s32[]{:S(2)}) async-start(), calls=%async_computation.4 | async-start | bytes 1880064 | tf_op jit(solution)/shard_map/all_gather | solution.py:46
  13.8 3.4 %copy-start.1 = (bf16[128,256]{1,0:T(8,128)(2,1)S(1)}, bf16[128,256]{1,0:T(8,128)(2,1)}, u32[]{:S(2)}) copy-start(bf16[128,256]{1,0:T(8,128)(2,1)} %param.7) | copy-start | bytes 196612
  55.4 1.0 copy-start.4
  115.0 64.7 %copy-start.5 = (bf16[1,256,768]{2,1,0:T(8,128)(2,1)S(1)}, bf16[1,256,768]{2,1,0:T(8,128)(2,1)}, u32[]{:S(2)}) copy-start(bf16[1,256,768]{2,1,0:T(8,128)(2,1)} %param.12) | copy-start | bytes 1179652
  178.2 3.1 %copy-start.3 = (bf16[768,1152]{1,0:T(8,128)(2,1)S(1)}, bf16[768,1152]{1,0:T(8,128)(2,1)}, u32[]{:S(2)}) copy-start(bf16[768,1152]{1,0:T(8,128)(2,1)} %all-gather.2.cloned.1.call-done) | copy-start | bytes 5308420
  183.6 41.2 %all-to-all-start.2 = ((bf16[64,6,512]{2,1,0:T(8,128)(2,1)}), bf16[64,6,512]{2,1,0:T(8,128)(2,1)S(1)}, u32[]{:S(2)}, u32[]{:S(2)}) async-start(bf16[64,6,512]{2,1,0:T(8,128)(2,1)} %pad_maximum_fusion.1), calls=%async_computation.2 | async-start | bytes 1048576 | tf_op jit(solution)/shard_map/all_to_all | solution.py:15
  224.9 6.1 %copy-start.6 = (bf16[128,2,1]{1,2,0:T(2,128)(2,1)S(1)}, bf16[128,2,1]{1,2,0:T(2,128)(2,1)}, u32[]{:S(2)}) copy-start(bf16[128,2,1]{1,2,0:T(2,128)(2,1)} %copy.31) | copy-start | bytes 1540
  227.1 11.2 %all-to-all-start.3 = ((f32[16,128,2]{1,2,0:T(2,128)}), f32[16,128,2]{1,2,0:T(2,128)S(1)}, u32[]{:S(2)}, u32[]{:S(2)}) async-start(f32[16,128,2]{1,2,0:T(2,128)} %broadcast_in_dim.50), calls=%async_computation.3 | async-start | bytes 32768 | tf_op jit(solution)/shard_map/all_to_all | solution.py:58
Sparse Core Ops, SparseCore 0:
  116.1 61.9 all-gather.1
where the time goes:
time: 248 us; the launch traced here: 246 us
  blocking collectives  91.5 us (37%)
  waiting for transfers between devices  81.1 us (33%)
  starting transfers between devices  26.2 us (11%)
  local copies, waits for them, and re-layouts  16.9 us (7%)
  between operations  14.4 us (6%)
  matrix products  10.3 us (4%)
  other arithmetic  5.52 us (2%)
    all_gather x1, waiting for transfers between devices, gather_turned(): result = lax.all_gather(both, axis, axis=0, tiled=True)  62.2 us
    all_to_all x1, blocking collectives, summed_on_arrival(): lax.all_to_all(split_up(shard, dim, devices), axis, 0, 0, tiled=True)  55.9 us
    all_to_all x1, blocking collectives, in_one_piece(): lax.all_to_all(both, axis, split_axis=split_dim, concat_axis=concat_dim,...  35.6 us
    all_to_all x1, starting transfers between devices, in_one_piece(): lax.all_to_all(both, axis, split_axis=split_dim, concat_axis=concat_dim,...  22.3 us
    all_to_all x1, waiting for transfers between devices, in_one_piece(): lax.all_to_all(both, axis, split_axis=split_dim, concat_axis=concat_dim,...  14.6 us
  transfers between devices with their start and end apart: 3, of which 3 were waited for; matrix products, arithmetic and copies ran while one was open for 3% of the time, Pallas kernels for 0%

commit v1 on v0

v1 whole, which is shorter than its diff:
```python
import functools

import jax
import jax.numpy as jnp
from jax import lax
from jax.experimental import pallas as pl
from jax.experimental.pallas import tpu as pltpu
from jax.sharding import PartitionSpec as P

MESH = pl.DeviceIdType.MESH
F32, BF16 = jnp.float32, jnp.bfloat16
PAD = 8


def dot(a, b, ca=1, cb=0):
    return lax.dot_general(a, b, (((ca,), (cb,)), ((), ())), preferred_element_type=F32)


def one_hot(flag):
    return jnp.where(flag, 1.0, 0.0).astype(BF16)


def iota(shape, dim):
    return lax.broadcasted_iota(jnp.int32, shape, dim).astype(F32)


def kernel(
    n_dp, n_expert, capacity,
    tok, go, ids, ids_t, rw, gw_hbm, uw_hbm, dw_hbm,
    mixed, gtok, groute, gg_hbm, gu_hbm, gd_hbm,
    gw, uw, dw, snd, rcv, xr, cr, part, ring_in, ring_out, x_out, x_in, act, rd,
    snd2, rcv2, gg, gu, gd,
    w_sem, a_sem, rs_send, rs_recv, x_sem, ag_send, ag_recv, rd_send, rd_recv, o_sem,
):
    nz = n_dp // 2
    rows = n_expert * capacity
    slab = rows // nz
    per_slab = n_expert // nz
    padded = n_expert * PAD
    half = part.shape[-1]
    feat = tok.shape[1]
    toks = tok.shape[0]
    me_dp, me = lax.axis_index("dp"), lax.axis_index("expert")
    xl, z = me_dp // nz, lax.rem(me_dp, nz)
    ahead = (xl * nz + lax.rem(z + 1, nz), me)
    behind = (xl * nz + lax.rem(z + nz - 1, nz), me)
    partner = ((1 - xl) * nz + z, me)
    toward = (ahead, behind)

    n_core = 2
    n_xh = 4 if n_expert == 64 else 1
    n_y = n_expert // (n_core * n_xh)
    core, y, xh = lax.rem(me, n_core), lax.rem(me // n_core, n_y), me // (n_core * n_y)

    def peer(i):
        d_xh = lax.rem(i, n_xh)
        d_core = lax.rem(i // n_xh, n_core)
        d_y = i // (n_xh * n_core)
        return (
            lax.rem(xh + d_xh, n_xh) * (n_core * n_y)
            + lax.rem(y + d_y, n_y) * n_core
            + lax.rem(core + d_core, n_core)
        )

    loads = [
        pltpu.make_async_copy(gw_hbm, gw, w_sem.at[0]),
        pltpu.make_async_copy(uw_hbm, uw, w_sem.at[1]),
        pltpu.make_async_copy(dw_hbm, dw, w_sem.at[2]),
    ]
    for c in loads:
        c.start()

    barrier = pltpu.get_barrier_semaphore()
    for who in (ahead, behind, partner):
        pl.semaphore_signal(barrier, inc=1, device_id=who, device_id_type=MESH)

    @pl.loop(1, n_expert)
    def _(i):
        pl.semaphore_signal(barrier, inc=1, device_id=(me_dp, peer(i)), device_id_type=MESH)

    expert_row = iota((n_expert, toks), 0)
    hot_t = [jnp.where(ids_t[k : k + 1, :].astype(F32) == expert_row, 1.0, 0.0) for k in range(2)]
    earlier_t = one_hot(iota((toks, toks), 0) < iota((toks, toks), 1))
    before_t = dot((hot_t[0] + hot_t[1]).astype(BF16), earlier_t)
    slot_rows = iota((padded, toks), 0)
    take_t = []
    for k in range(2):
        pos = jnp.sum(before_t * hot_t[k], axis=0, keepdims=True)
        slot = ids_t[k : k + 1, :].astype(F32) * PAD + pos
        take_t.append(one_hot(slot_rows == slot))

    tokens = tok[...]
    grads = go[...].astype(F32)
    p = [rw[:, k : k + 1] for k in range(2)]
    send_x = dot(take_t[0] + take_t[1], tokens)
    send_c = dot(take_t[0], (p[0] * grads).astype(BF16)) + dot(take_t[1], (p[1] * grads).astype(BF16))
    snd[:, :, :feat] = send_x.reshape(n_expert, PAD, feat).astype(BF16)
    snd[:, :, feat:] = send_c.reshape(n_expert, PAD, feat).astype(BF16)

    pl.semaphore_wait(barrier, n_expert - 1 + 3)

    def exchange(src, dst, s):
        @pl.loop(1, n_expert)
        def _(i):
            to = peer(i)
            pltpu.make_async_remote_copy(
                src_ref=src.at[to], dst_ref=dst.at[me],
                send_sem=a_sem.at[2 * s], recv_sem=a_sem.at[2 * s + 1],
                device_id=(me_dp, to), device_id_type=MESH,
            ).start()

        dst[me] = src[me]

    def exchange_all(src, dst, s):
        return pltpu.make_async_remote_copy(
            src_ref=src.at[pl.ds(0, n_expert - 1)], dst_ref=dst.at[pl.ds(0, n_expert - 1)],
            send_sem=a_sem.at[2 * s], recv_sem=a_sem.at[2 * s + 1],
            device_id=partner, device_id_type=MESH,
        )

    exchange(snd, rcv, 0)

    expert_col = iota((toks, n_expert), 1)
    hot = [jnp.where(ids[:, k : k + 1].astype(F32) == expert_col, 1.0, 0.0) for k in range(2)]
    earlier = one_hot(iota((toks, toks), 1) < iota((toks, toks), 0))
    before = dot(earlier, (hot[0] + hot[1]).astype(BF16))
    slot_cols = iota((toks, padded), 1)
    take, take_dot, pos_col = [], [], []
    for k in range(2):
        base = ids[:, k : k + 1].astype(F32) * PAD
        pos_col.append(jnp.sum(before * hot[k], axis=1, keepdims=True))
        take.append(one_hot(slot_cols == base + pos_col[k]))
        take_dot.append(one_hot(slot_cols == base + capacity))

    r_col = iota((rows, 1), 0)
    group = jnp.floor((r_col + 0.5) / capacity)
    shrink = one_hot(iota((rows, padded), 1) == r_col + (PAD - capacity) * group)
    g_col = iota((padded, 1), 0)
    g_group = jnp.floor((g_col + 0.5) / PAD)
    g_left = g_col - PAD * g_group
    g_row = jnp.where(g_left < capacity, capacity * g_group + g_left, -1.0)
    grow = one_hot(iota((padded, rows), 1) == g_row)
    dot_row = jnp.where(g_left == capacity, jnp.floor((g_group + 0.5) / per_slab), -1.0)
    place_dot = one_hot(iota((padded, 16), 1) == dot_row)

    for c in loads:
        c.wait()
    exchange_all(snd, rcv, 0).wait_recv()
    for at, ref in ((0, xr), (feat, cr)):
        arrived = rcv[:, :, at : at + feat].reshape(padded, feat)
        ref[...] = dot(shrink, arrived).astype(BF16)

    for a, value in enumerate(
        (lambda: dot(xr[...], gw[...]), lambda: dot(xr[...], uw[...]), lambda: dot(cr[...], dw[...], 1, 1))
    ):
        full = value().astype(BF16)
        for h in range(2):
            part[h, a] = full[:, h * half : (h + 1) * half].reshape(nz, slab, half)

    long, short = nz // 2, nz // 2 - 1
    hops = ((long, short), (short, long))
    column = (1 - xl, xl)
    sent = []

    def rs_copy(d, o, s, src):
        return pltpu.make_async_remote_copy(
            src_ref=src, dst_ref=ring_in.at[d, o, s],
            send_sem=rs_send.at[d, o, s], recv_sem=rs_recv.at[d, o, s],
            device_id=toward[d], device_id_type=MESH,
        )

    arriving = {}
    for s in range(long):
        for o in range(2):
            for d in range(2):
                length = hops[d][o]
                if s >= length:
                    continue
                far = length - s
                dest = lax.rem(z + far, nz) if d == 0 else lax.rem(z + nz - far, nz)
                if s == 0:
                    src = part.at[column[o], :, dest]
                else:
                    arriving[d, o].wait_recv()
                    ring_out[d, o, s - 1] = (
                        ring_in[d, o, s - 1].astype(F32) + part[column[o], :, dest].astype(F32)
                    ).astype(BF16)
                    src = ring_out.at[d, o, s - 1]
                c = rs_copy(d, o, s, src)
                c.start()
                sent.append(c)
                arriving[d, o] = c

    def total(o):
        value = part[column[o], :, z].astype(F32)
        for d in range(2):
            if hops[d][o]:
                arriving[d, o].wait_recv()
                value = value + ring_in[d, o, hops[d][o] - 1].astype(F32)
        return value

    x_out[...] = total(0).astype(BF16)
    to_partner = pltpu.make_async_remote_copy(
        src_ref=x_out, dst_ref=x_in, send_sem=x_sem.at[0], recv_sem=x_sem.at[1],
        device_id=partner, device_id_type=MESH,
    )
    to_partner.start()
    sent.append(to_partner)
    own = total(1)
    to_partner.wait_recv()
    own = own + x_in[...].astype(F32)

    gate, up, back = own[0], own[1], own[2]
    sig = jax.nn.sigmoid(gate)
    swished = gate * sig
    hidden = swished * up
    act[xl, 0, z] = hidden.astype(BF16)
    act[xl, 1, z] = (back * up * sig * (1.0 + gate * (1.0 - sig))).astype(BF16)
    act[xl, 2, z] = (back * swished).astype(BF16)
    sums = jnp.sum(hidden * back, axis=1, keepdims=True)
    diagonal = iota((slab, 128), 0) == iota((slab, 128), 1)
    rd[xl, z] = jnp.broadcast_to(
        jnp.sum(jnp.where(diagonal, sums, 0.0), axis=0, keepdims=True), (8, 128)
    )

    def pair_of_copies(src_h, src_z, sems, who):
        return (
            pltpu.make_async_remote_copy(
                src_ref=act.at[src_h, :, src_z], dst_ref=act.at[src_h, :, src_z],
                send_sem=ag_send.at[sems], recv_sem=ag_recv.at[sems],
                device_id=who, device_id_type=MESH,
            ),
            pltpu.make_async_remote_copy(
                src_ref=rd.at[src_h, src_z], dst_ref=rd.at[src_h, src_z],
                send_sem=rd_send.at[sems], recv_sem=rd_recv.at[sems],
                device_id=who, device_id_type=MESH,
            ),
        )

    def go_on(copies):
        for c in copies:
            c.start()
            sent.append(c)
        return copies

    def landed(copies):
        for c in copies:
            c.wait_recv()

    ag_column = (xl, 1 - xl)
    swap = go_on(pair_of_copies(xl, z, 4 * nz, partner))
    coming = {}
    for s in range(long):
        for o in range(2):
            for d in range(2):
                if s >= hops[d][o]:
                    continue
                if s == 0:
                    if o == 1 and d == 0:
                        landed(swap)
                    elif o == 1 and not hops[0][1]:
                        landed(swap)
                else:
                    landed(coming[d, o])
                source = lax.rem(z + nz - s, nz) if d == 0 else lax.rem(z + s, nz)
                coming[d, o] = go_on(
                    pair_of_copies(ag_column[o], source, (d * 2 + o) * nz + s, toward[d])
                )
    for key in coming:
        landed(coming[key])

    full = [
        jnp.concatenate([act[h, a].reshape(rows, half) for h in range(2)], axis=1) for a in range(3)
    ]
    hid, g_grad, u_grad = full
    out_rows = dot(hid, dw[...]).astype(BF16)
    in_rows = (dot(g_grad, gw[...], 1, 1) + dot(u_grad, uw[...], 1, 1)).astype(BF16)
    dots = jnp.concatenate([rd[0, j, 0:1, :] + rd[1, j, 0:1, :] for j in range(nz)], axis=0)
    dots = jnp.concatenate([dots, jnp.zeros((16 - nz, 128), F32)], axis=0)
    parts = []
    for _ in range(3):
        piece = dots.astype(BF16)
        parts.append(piece)
        dots = dots - piece.astype(F32)
    placed = [dot(place_dot, piece) for piece in parts]
    width = 2 * feat
    for at, value in ((0, out_rows), (feat, in_rows)):
        spread = dot(grow, value)
        pieces = []
        for c in range(0, feat, 128):
            k = (at + c) // 128
            block = spread[:, c : c + 128]
            pieces.append(block + placed[k] if k < 3 else block)
        spread = jnp.concatenate(pieces, axis=1)
        snd2[:, :, at : at + feat] = spread.reshape(n_expert, PAD, feat).astype(BF16)
    exchange(snd2, rcv2, 1)

    gg[...] = dot(xr[...], g_grad, 0, 0).astype(BF16)
    gu[...] = dot(xr[...], u_grad, 0, 0).astype(BF16)
    gd[...] = dot(hid, cr[...], 0, 0).astype(BF16)
    stores = [
        pltpu.make_async_copy(gg, gg_hbm, o_sem.at[0]),
        pltpu.make_async_copy(gu, gu_hbm, o_sem.at[1]),
        pltpu.make_async_copy(gd, gd_hbm, o_sem.at[2]),
    ]
    for c in stores:
        c.start()
    for c in sent:
        c.wait_send()
    exchange_all(snd, rcv, 0).wait_send()

    exchange_all(snd2, rcv2, 1).wait_recv()
    back_out = rcv2[:, :, :feat].reshape(padded, feat)
    back_in = rcv2[:, :, feat:].reshape(padded, feat)
    mixed[...] = (p[0] * dot(take[0], back_out) + p[1] * dot(take[1], back_out)).astype(BF16)
    gtok[...] = dot(take[0] + take[1], back_in).astype(BF16)
    lane = iota((toks, 128), 1)
    first = (lax.rem(me, per_slab) * capacity).astype(F32)
    cols = []
    for k in range(2):
        low = dot(take_dot[k], back_out)
        high = dot(take_dot[k], back_in[:, :128])
        picked = low[:, :128] + low[:, 128:256] + high
        mine = jnp.where(lane == first + pos_col[k], picked, 0.0)
        cols.append(jnp.sum(mine, axis=1, keepdims=True) / p[k])
    groute[:, 0:1] = cols[0]
    groute[:, 1:2] = cols[1]
    exchange_all(snd2, rcv2, 1).wait_send()
    for c in stores:
        c.wait()


def local(n_dp, n_expert, tokens, grad_out, expert_ids, route_weights, gate_weight, up_weight, down_weight):
    toks, feat = tokens.shape
    top = expert_ids.shape[1]
    hid = gate_weight.shape[2]
    half = hid // 2
    nz = n_dp // 2
    capacity = max(2, 3 * toks * top // (2 * n_expert))
    rows = n_expert * capacity
    slab = rows // nz
    vmem = pl.BlockSpec(memory_space=pltpu.VMEM)
    hbm = pl.BlockSpec(memory_space=pl.ANY)
    block = (3, slab, half)
    width = 2 * feat
    wire = (n_expert, PAD, width)
    dma = pltpu.SemaphoreType.DMA
    out = pl.pallas_call(
        functools.partial(kernel, n_dp, n_expert, capacity),
        out_shape=(
            jax.ShapeDtypeStruct((toks, feat), BF16),
            jax.ShapeDtypeStruct((toks, feat), BF16),
            jax.ShapeDtypeStruct((toks, top), F32),
            jax.ShapeDtypeStruct((feat, hid), BF16),
            jax.ShapeDtypeStruct((feat, hid), BF16),
            jax.ShapeDtypeStruct((hid, feat), BF16),
        ),
        in_specs=[vmem] * 5 + [hbm] * 3,
        out_specs=(vmem, vmem, vmem, hbm, hbm, hbm),
        scratch_shapes=[
            pltpu.VMEM((feat, hid), BF16),
            pltpu.VMEM((feat, hid), BF16),
            pltpu.VMEM((hid, feat), BF16),
            pltpu.VMEM(wire, BF16),
            pltpu.VMEM(wire, BF16),
            pltpu.VMEM((rows, feat), BF16),
            pltpu.VMEM((rows, feat), BF16),
            pltpu.VMEM((2, 3, nz, slab, half), BF16),
            pltpu.VMEM((2, 2, nz // 2, *block), BF16),
            pltpu.VMEM((2, 2, max(1, nz // 2 - 1), *block), BF16),
            pltpu.VMEM(block, BF16),
            pltpu.VMEM(block, BF16),
            pltpu.VMEM((2, 3, nz, slab, half), BF16),
            pltpu.VMEM((2, nz, 8, 128), F32),
            pltpu.VMEM(wire, BF16),
            pltpu.VMEM(wire, BF16),
            pltpu.VMEM((feat, hid), BF16),
            pltpu.VMEM((feat, hid), BF16),
            pltpu.VMEM((hid, feat), BF16),
            dma((3,)),
            dma((4,)),
            dma((2, 2, nz // 2)),
            dma((2, 2, nz // 2)),
            dma((2,)),
            dma((4 * nz + 1,)),
            dma((4 * nz + 1,)),
            dma((4 * nz + 1,)),
            dma((4 * nz + 1,)),
            dma((3,)),
        ],
        compiler_params=pltpu.CompilerParams(
            collective_id=0, has_side_effects=True, vmem_limit_bytes=40 * 1024 * 1024
        ),
        name="routed_layer",
    )(
        tokens, grad_out, expert_ids, expert_ids.T, route_weights,
        gate_weight.reshape(feat, hid), up_weight.reshape(feat, hid), down_weight.reshape(hid, feat),
    )
    mixed, gtok, groute, gg, gu, gd = out
    return mixed, gtok, groute, gg[None], gu[None], gd[None]


def solution(mesh):
    placed = (
        P("expert", "dp"),
        P("expert", "dp"),
        P("expert", None),
        P("expert", None),
        P("expert", "dp", None),
        P("expert", "dp", None),
        P("expert", None, "dp"),
    )
    return jax.shard_map(
        functools.partial(local, mesh.shape["dp"], mesh.shape["expert"]),
        mesh=mesh,
        in_specs=placed,
        out_specs=(
            P("expert", "dp"),
            P("expert", "dp"),
            P("expert", None),
            P("expert", "dp", None),
            P("expert", "dp", None),
            P("expert", None, "dp"),
        ),
        check_vma=False,
    )
```

time: 248 us -> 114 us (0.46)
  Pallas kernels: 0 us -> 104 us
  blocking collectives: 91.5 us -> 0 us
  waiting for transfers between devices: 81.1 us -> 0 us
  starting transfers between devices: 26.2 us -> 0 us
  between operations: 14.4 us -> 0.67 us
  matrix products: 10.3 us -> 0 us
  local copies, waits for them, and re-layouts: 16.9 us -> 8.65 us
  other arithmetic: 5.52 us -> 0 us
    pallas_call x0 -> x1, Pallas kernels: none -> 104 us  [local(): pl.pallas_call(functools.partial(kernel, n_dp, n_expert, capacity), out_s...]
    all_to_all x2 -> x0, blocking collectives: 91.5 us -> none  [the longest x1 55.9 us: summed_on_arrival(): lax.all_to_all(split_up(shard, dim, devices), axis, 0, 0, tiled=True)]
    all_gather x1 -> x0, waiting for transfers between devices: 62.2 us -> none  [gather_turned(): result = lax.all_gather(both, axis, axis=0, tiled=True)]
    all_to_all x2 -> x0, starting transfers between devices: 26.2 us -> none  [the longest x1 22.3 us: in_one_piece(): lax.all_to_all(both, axis, split_axis=split_dim, concat_axis=concat_dim,...]
    all_to_all x2 -> x0, waiting for transfers between devices: 18.9 us -> none  [the longest x1 14.6 us: in_one_piece(): lax.all_to_all(both, axis, split_axis=split_dim, concat_axis=concat_dim,...]
    dot_general x11 -> x0, matrix products: 10.3 us -> none  [the longest x1 1.55 us: local(): jnp.einsum('erh,edh->erd', gate_grad, gate_weight, preferred_element_type...]
    gather x6 -> x0, local copies, waits for them, and re-layouts: 9.29 us -> none  [the longest x1 2.81 us: local(): route_weights.reshape(-1)[source][:, None]]
    unnamed x19 -> x22, local copies, waits for them, and re-layouts: 1.99 us -> 8.65 us
  transfers between devices with their start and end apart: 3 -> 0, of which waited for: 3 -> 0; matrix products, arithmetic and copies ran while one was open for 3% -> 0% of each run, Pallas kernels for 0% -> 0%
where the time goes in v1:
time: 114 us; the launch traced here: 113 us
  Pallas kernels  104 us (91%)
  local copies, waits for them, and re-layouts  8.65 us (8%)
    pallas_call x1, Pallas kernels, local(): pl.pallas_call(functools.partial(kernel, n_dp, n_expert, capacity), out_s...  104 us
    unnamed x22, local copies, waits for them, and re-layouts  8.65 us

profile of v1, /device:TPU:1, one launch (start us, length us, event | category | flops | bytes accessed | tf_op | source)
XLA Modules:
  0.0 113.3 jit_solution(8210603565532199772)
XLA Ops:
  0.6 0.0 copy-start.6
  0.6 0.0 copy-start.5
  0.7 0.7 copy-done.6
  1.3 0.0 copy-start.3
  1.3 0.0 copy-start.4
  1.3 0.1 copy.14.rw
  1.4 0.0 copy-done.5
  1.4 0.1 copy.13.ids
  1.5 0.6 copy-done.3
  2.2 0.0 copy-done.4
  2.2 0.0 copy-start
  2.2 1.0 copy-done
  3.2 0.0 copy-start.1
  3.2 1.0 copy-done.1
  4.2 0.0 copy-start.2
  4.2 1.0 copy-done.2
  5.2 103.9 %routed_layer.1 = (bf16[128,256]{1,0:T(8,128)(2,1)S(1)}, bf16[128,256]{1,0:T(8,128)(2,1)S(1)}, f32[128,2]{1,0:T(8,128)S(1)}, bf16[256,768]{1,0:T(8,128)(2,1)S(1)...) custom-call(bf16[128,256]{1,0:T(8,128)(2,1)S(1)} %copy-done.3, bf16[128,256]{1,0:T(8,128)(2,1)S(1)} %copy-done.4, ...), custom_call_target="tpu_custom_call" | custom-call | tf_op jit(solution)/shard_map/routed_layer/pallas_call | solution.py:348
  109.1 0.6 copy.15
  109.8 0.6 copy.21
  110.4 0.6 copy.22
  111.0 0.7 copy.23
  111.8 0.7 copy.24
  112.5 0.7 copy.25
Async XLA Ops:
  0.6 0.7 copy-start.6
  0.6 0.8 copy-start.5
  1.3 0.8 copy-start.3
  1.3 0.9 copy-start.4
  2.2 1.0 copy-start
  3.2 1.0 copy-start.1
  4.2 1.0 copy-start.2

commit v2 on v1

v2 whole, which is shorter than its diff:
```python
import functools

import jax
import jax.numpy as jnp
from jax import lax
from jax.experimental import pallas as pl
from jax.experimental.pallas import tpu as pltpu
from jax.sharding import PartitionSpec as P

MESH = pl.DeviceIdType.MESH
F32, BF16 = jnp.float32, jnp.bfloat16
PAD = 8
LANES = 128

GATE_OTHER, GATE_OWN, UP_OWN, BACK_OTHER, BACK_OWN, BACK_LAST = range(6)
SUMS = (
    (False, 0, 3, False, 1),
    (True, 0, 3, False, 0),
    (True, 3, 3, True, 1),
    (False, 6, 2, False, 0),
    (True, 6, 2, False, 0),
    (True, 8, 1, True, 1),
)
HID_OWN, HID_OTHER, GRAD_OWN, GRAD_OTHER = range(4)
GATHERS = ((True, 0, 3, 0), (False, 0, 2, 1), (True, 3, 6, 1), (False, 3, 3, 0))
ACROSS = {HID_OWN: (2, 1), GRAD_OWN: (6, 3)}


def dot(a, b, ca=1, cb=0):
    return lax.dot_general(a, b, (((ca,), (cb,)), ((), ())), preferred_element_type=F32)


def one_hot(flag):
    return jnp.where(flag, 1.0, 0.0).astype(BF16)


def iota(shape, dim):
    return lax.broadcasted_iota(jnp.int32, shape, dim).astype(F32)


def kernel(
    n_dp, n_expert, capacity,
    tok_hbm, go_hbm, ids_hbm, rw_hbm, gw_hbm, uw_hbm, dw_hbm,
    mixed_hbm, gtok_hbm, groute_hbm, gg_hbm, gu_hbm, gd_hbm,
    tok, go, ids, rw, gw, uw, dw,
    snd, rcv, snd_o, rcv_o, snd_i, rcv_i, snd_r, rcv_r, xr, cr,
    mixed, gtok, groute, gg, gu, gd,
    part, ring_in, ring_out, x_in, swap_out, swap_in, act, rd,
    in_sem, out_sem, a_sem, rs_send, rs_recv, x_send, x_recv, swap_send, swap_recv,
    ag_send, ag_recv, cross_send, cross_recv, rd_send, rd_recv, rdx_send, rdx_recv, first_send, first_recv,
):
    nz = n_dp // 2
    rows = n_expert * capacity
    slab = rows // nz
    per_slab = n_expert // nz
    padded = n_expert * PAD
    feat, toks = tok.shape[1], tok.shape[0]
    me_dp, me = lax.axis_index("dp"), lax.axis_index("expert")
    xl, z = me_dp // nz, lax.rem(me_dp, nz)
    ahead = (xl * nz + lax.rem(z + 1, nz), me)
    behind = (xl * nz + lax.rem(z + nz - 1, nz), me)
    partner = ((1 - xl) * nz + z, me)
    toward = (ahead, behind)
    half_of = {True: xl, False: 1 - xl}

    loads = [
        pltpu.make_async_copy(src, dst, in_sem.at[i])
        for i, (src, dst) in enumerate(
            ((ids_hbm, ids), (rw_hbm, rw), (tok_hbm, tok), (go_hbm, go), (gw_hbm, gw), (uw_hbm, uw), (dw_hbm, dw))
        )
    ]
    for c in loads:
        c.start()

    n_core = 2
    n_xh = 4 if n_expert == 64 else 1
    n_y = n_expert // (n_core * n_xh)
    core, y, xh = lax.rem(me, n_core), lax.rem(me // n_core, n_y), me // (n_core * n_y)
    nearby = [
        lax.rem(xh + d_xh, n_xh) * (n_core * n_y) + lax.rem(core + d_core, n_core)
        for d_core in range(n_core)
        for d_xh in range(n_xh)
    ]

    def each_peer(act_on):
        def at(i, skip):
            d_y = n_y // 2 + (1 - 2 * (i % 2)) * ((i + 1) // 2)
            base = lax.rem(y + d_y, n_y) * n_core
            for there in nearby[skip:]:
                act_on(base + there)

        @pl.loop(0, n_y - 1)
        def _(i):
            at(i, 0)

        at(n_y - 1, 1)

    barrier = pltpu.get_barrier_semaphore()
    for who in (ahead, behind, partner):
        pl.semaphore_signal(barrier, inc=1, device_id=who, device_id_type=MESH)
    each_peer(lambda to: pl.semaphore_signal(barrier, inc=1, device_id=(me_dp, to), device_id_type=MESH))

    loads[0].wait()
    loads[1].wait()
    ids_row = ids[...].astype(F32)
    flat = jnp.concatenate([ids_row, rw[...], jnp.zeros((toks - 4, toks), F32)], axis=0)
    turned = flat.T
    expert_row = iota((n_expert, toks), 0)
    hot_t = [jnp.where(ids_row[k : k + 1, :] == expert_row, 1.0, 0.0) for k in range(2)]
    earlier_t = one_hot(iota((toks, toks), 0) < iota((toks, toks), 1))
    before_t = dot((hot_t[0] + hot_t[1]).astype(BF16), earlier_t)
    slot_rows = iota((rows, toks), 0)
    take_t = []
    for k in range(2):
        pos = jnp.sum(before_t * hot_t[k], axis=0, keepdims=True)
        take_t.append(one_hot(slot_rows == ids_row[k : k + 1, :] * capacity + pos))
    p = [turned[:, 2 + k : 3 + k] for k in range(2)]
    blocks = 2 * feat // LANES
    per_group = PAD // 2 if n_expert < PAD else PAD
    height = per_group * capacity
    tall = blocks * height
    packs = blocks * capacity // PAD
    to_row = iota((tall, 1), 0)
    block = jnp.floor((to_row + 0.5) / height)
    inner = to_row - height * block
    which = jnp.floor((inner + 0.5) / capacity)
    target = which * (blocks * capacity) + block * capacity + (inner - capacity * which)
    unpack = one_hot(iota((tall, tall), 1) == target)
    from_row = iota((1, tall), 1)
    block = jnp.floor((from_row + 0.5) / height)
    inner = from_row - height * block
    which = jnp.floor((inner + 0.5) / capacity)
    source = which * (blocks * capacity) + block * capacity + (inner - capacity * which)
    pack = one_hot(iota((tall, tall), 0) == source)
    loads[2].wait()
    loads[3].wait()
    grads = go[...].astype(F32)
    send_x = dot(take_t[0] + take_t[1], tok[...]).astype(BF16)
    send_c = (dot(take_t[0], (p[0] * grads).astype(BF16)) + dot(take_t[1], (p[1] * grads).astype(BF16))).astype(BF16)
    for j in range(n_expert // per_group):
        lo = j * height
        stacked = jnp.concatenate(
            [v[lo : lo + height, c : c + LANES] for v in (send_x, send_c) for c in range(0, feat, LANES)], axis=0
        )
        snd[j * per_group : (j + 1) * per_group] = dot(pack, stacked).reshape(per_group, packs, PAD, LANES).astype(BF16)

    pl.semaphore_wait(barrier, n_expert - 1 + 3)

    def exchange(src, dst, s):
        def send(to):
            pltpu.make_async_remote_copy(
                src_ref=src.at[to], dst_ref=dst.at[me],
                send_sem=a_sem.at[2 * s], recv_sem=a_sem.at[2 * s + 1],
                device_id=(me_dp, to), device_id_type=MESH,
            ).start()

        each_peer(send)
        dst[me] = src[me]

    def exchange_all(src, dst, s):
        return pltpu.make_async_remote_copy(
            src_ref=src.at[pl.ds(0, n_expert - 1)], dst_ref=dst.at[pl.ds(0, n_expert - 1)],
            send_sem=a_sem.at[2 * s], recv_sem=a_sem.at[2 * s + 1],
            device_id=partner, device_id_type=MESH,
        )

    exchange(snd, rcv, 0)
    expert_col = iota((toks, n_expert), 1)
    hot = [jnp.where(turned[:, k : k + 1] == expert_col, 1.0, 0.0) for k in range(2)]
    earlier = one_hot(iota((toks, toks), 1) < iota((toks, toks), 0))
    before = dot(earlier, (hot[0] + hot[1]).astype(BF16))
    slot_cols = iota((toks, padded), 1)
    take, pos_col = [], []
    for k in range(2):
        base = turned[:, k : k + 1] * PAD
        pos_col.append(jnp.sum(before * hot[k], axis=1, keepdims=True))
        take.append(one_hot(slot_cols == base + pos_col[k]))

    g_col = iota((padded, 1), 0)
    g_group = jnp.floor((g_col + 0.5) / PAD)
    g_left = g_col - PAD * g_group
    g_row = jnp.where(g_left < capacity, capacity * g_group + g_left, -1.0)
    grow = one_hot(iota((padded, rows), 1) == g_row)

    long, short = nz // 2, nz // 2 - 1
    offsets = [long] + [sign * d for d in range(short, 0, -1) for sign in (1, -1)] + [0]
    sent = []

    def go_on(src, dst, send_sem, recv_sem, who):
        c = pltpu.make_async_remote_copy(
            src_ref=src, dst_ref=dst, send_sem=send_sem, recv_sem=recv_sem,
            device_id=who, device_id_type=MESH,
        )
        c.start()
        sent.append(c)
        return c

    def at_z(off):
        return lax.rem(z + nz + off, nz)

    x_late, x_seen, ring = {}, set(), {}

    def put_part(a, value):
        full = value.astype(BF16)
        for h in range(2):
            for u in range(3):
                lo = (3 * h + u) * LANES
                part[h, :, 3 * a + u] = full[:, lo : lo + LANES].reshape(nz, slab, LANES)

    def to_other(k):
        _, u0, n, _, _ = SUMS[k]
        for i, off in enumerate(offsets):
            x_late[k, off] = go_on(
                part.at[half_of[False], at_z(off), pl.ds(u0, n)], x_in.at[at_z(off), pl.ds(u0, n)],
                x_send.at[k, i], x_recv.at[k, i], partner,
            )

    def mine(k, off):
        here, u0, n, crossed, _ = SUMS[k]
        value = part[half_of[here], at_z(off), u0 : u0 + n].astype(F32)
        if crossed:
            x_late[k, off].wait_recv()
            value = value + x_in[at_z(off), u0 : u0 + n].astype(F32)
        return value

    def step(k, s):
        here, u0, n, crossed, far_way = SUMS[k]
        for d in range(2):
            length = long if d == far_way else short
            if s >= length:
                continue
            off = (length - s) * (1 - 2 * d)
            key = long if abs(off) == long else off
            units = pl.ds(u0, n)
            if s == 0 and not crossed:
                src = part.at[half_of[here], at_z(off), units]
            else:
                value = mine(k, key)
                if s:
                    ring[k, d].wait_recv()
                    value = value + ring_in[int(here), d, s - 1, u0 : u0 + n].astype(F32)
                ring_out[int(here), d, s, u0 : u0 + n] = value.astype(BF16)
                src = ring_out.at[int(here), d, s, units]
            ring[k, d] = go_on(
                src, ring_in.at[int(here), d, s, units], rs_send.at[k, d, s], rs_recv.at[k, d, s], toward[d]
            )

    def total(k):
        here, u0, n, _, far_way = SUMS[k]
        value = mine(k, 0)
        for d in range(2):
            length = long if d == far_way else short
            if length:
                ring[k, d].wait_recv()
                value = value + ring_in[int(here), d, length - 1, u0 : u0 + n].astype(F32)
        return value

    def swap(k):
        _, u0, n, _, _ = SUMS[k]
        units = pl.ds(u0, n)
        swap_out[u0 : u0 + n] = total(k).astype(BF16)
        return go_on(swap_out.at[units], swap_in.at[units], swap_send.at[k], swap_recv.at[k], partner)

    def swapped(k, c):
        _, u0, n, _, _ = SUMS[k]
        value = total(k)
        c.wait_recv()
        return value + swap_in[u0 : u0 + n].astype(F32)

    exchange_all(snd, rcv, 0).wait_recv()
    for j in range(n_expert // per_group):
        lo = j * height
        stacked = dot(unpack, rcv[j * per_group : (j + 1) * per_group].reshape(tall, LANES)).astype(BF16)
        for i, (ref, c) in enumerate((ref, c) for ref in (xr, cr) for c in range(0, feat, LANES)):
            ref[lo : lo + height, c : c + LANES] = stacked[i * height : (i + 1) * height]
    for c in loads[4:]:
        c.wait()
    put_part(0, dot(xr[...], gw[...]))
    step(GATE_OTHER, 0)
    step(GATE_OWN, 0)
    put_part(1, dot(xr[...], uw[...]))
    to_other(UP_OWN)
    put_part(2, dot(cr[...], dw[...], 1, 1))
    to_other(BACK_LAST)

    plan = (
        (BACK_OTHER, 0), (BACK_OWN, 0), (GATE_OTHER, 1), (UP_OWN, 0), (BACK_LAST, 0), (GATE_OWN, 1),
        (BACK_OTHER, 1), (BACK_OWN, 1), (GATE_OTHER, 2), (UP_OWN, 1), (BACK_LAST, 1), (GATE_OWN, 2),
        (BACK_OTHER, 2), (BACK_OWN, 2), (GATE_OTHER, 3), (UP_OWN, 2), (BACK_LAST, 2), (GATE_OWN, 3),
        (BACK_OTHER, 3), (BACK_OWN, 3), ("swap", GATE_OTHER), (UP_OWN, 3), (BACK_LAST, 3), ("swap", BACK_OTHER),
    )
    swaps = {}
    for what, s in plan:
        if what == "swap":
            swaps[s] = swap(s)
        elif s < long:
            step(what, s)

    gate = swapped(GATE_OWN, swaps[GATE_OTHER])
    up = total(UP_OWN)
    back = jnp.concatenate([swapped(BACK_OWN, swaps[BACK_OTHER]), total(BACK_LAST)], axis=0)
    sig = jax.nn.sigmoid(gate)
    swished = gate * sig
    hidden = swished * up
    act[xl, z, 0:3] = hidden.astype(BF16)
    act[xl, z, 3:6] = (back * up * sig * (1.0 + gate * (1.0 - sig))).astype(BF16)
    act[xl, z, 6:9] = (back * swished).astype(BF16)
    sums = jnp.sum(jnp.sum(hidden * back, axis=0), axis=1, keepdims=True)
    diagonal = iota((slab, LANES), 0) == iota((slab, LANES), 1)
    rd[xl, z] = jnp.broadcast_to(
        jnp.sum(jnp.where(diagonal, sums, 0.0), axis=0, keepdims=True), (8, LANES)
    )

    own, other = half_of[True], half_of[False]
    comes, crossing = {}, {HID_OWN: [], GRAD_OWN: []}

    def ring_send(k, s, d):
        here, u0, n, far_way = GATHERS[k]
        where = at_z(s if d else -s)
        h, units = half_of[here], pl.ds(u0, n)
        both = [
            go_on(act.at[h, where, units], act.at[h, where, units], ag_send.at[k, d, s], ag_recv.at[k, d, s], toward[d])
        ]
        if k == HID_OWN:
            both.append(go_on(rd.at[h, where], rd.at[h, where], rd_send.at[d, s], rd_recv.at[d, s], toward[d]))
        comes[k, d] = both

    def cross(k, s, d):
        where = at_z(s if d else -s)
        u0, n = ACROSS[k]
        units = pl.ds(u0, n)
        j = int(k == GRAD_OWN)
        crossing[k].append(
            go_on(act.at[own, where, units], act.at[own, where, units], cross_send.at[j, d, s], cross_recv.at[j, d, s], partner)
        )
        if k == HID_OWN:
            crossing[k].append(go_on(rd.at[own, where], rd.at[own, where], rdx_send.at[d, s], rdx_recv.at[d, s], partner))

    def ag_step(k, s):
        here, _, _, far_way = GATHERS[k]
        for d in range(2):
            length = long if d == far_way else short
            if s > length or (s == length and not here) or (s and (k, d) not in comes):
                continue
            if s:
                for c in comes[k, d]:
                    c.wait_recv()
            if s < length:
                ring_send(k, s, d)
            if s and here:
                cross(k, s, d)

    def ag_last(k):
        _, _, _, far_way = GATHERS[k]
        for d in range(2):
            if (k, d) in comes:
                for c in comes[k, d]:
                    c.wait_recv()

    firsts = {}

    def first(k, u0, n):
        units = pl.ds(u0, n)
        j = int(k == GRAD_OWN)
        firsts[k] = [
            go_on(act.at[own, z, units], act.at[own, z, units], first_send.at[j], first_recv.at[j], partner)
        ]
        if k == HID_OWN:
            firsts[k].append(go_on(rd.at[own, z], rd.at[own, z], first_send.at[2], first_recv.at[2], partner))

    first(HID_OWN, 0, 3)
    ag_step(HID_OWN, 0)
    first(GRAD_OWN, 3, 6)
    for job in (
        (HID_OWN, 1), "hid", (HID_OTHER, 0), (GRAD_OWN, 0), "grad", (GRAD_OTHER, 0),
        (HID_OWN, 2), (HID_OTHER, 1), (GRAD_OWN, 1), (GRAD_OTHER, 1),
        (HID_OWN, 3), (HID_OTHER, 2), (GRAD_OWN, 2), (GRAD_OTHER, 2),
        (HID_OWN, 4), (HID_OTHER, 3), (GRAD_OWN, 3), (GRAD_OTHER, 3), (GRAD_OWN, 4),
    ):
        if job in ("hid", "grad"):
            for c in firsts[HID_OWN if job == "hid" else GRAD_OWN]:
                c.wait_recv()
        elif job[1] <= long:
            ag_step(*job)
    ag_last(HID_OTHER)
    for c in crossing[HID_OWN]:
        c.wait_recv()

    def whole(a):
        return jnp.concatenate(
            [act[h, :, 3 * a + u].reshape(rows, LANES) for h in range(2) for u in range(3)], axis=1
        )

    hid = whole(0)
    out_rows = dot(hid, dw[...]).astype(BF16)
    for j in range(nz):
        snd_r[j] = rd[0, j, 0:1, :] + rd[1, j, 0:1, :]
    spread = dot(grow, out_rows)
    snd_o[...] = spread.reshape(n_expert, PAD, feat).astype(BF16)
    exchange(snd_o, rcv_o, 2)

    def send_dots(to):
        pltpu.make_async_remote_copy(
            src_ref=snd_r.at[to // per_slab], dst_ref=rcv_r.at[me],
            send_sem=a_sem.at[2], recv_sem=a_sem.at[3],
            device_id=(me_dp, to), device_id_type=MESH,
        ).start()

    each_peer(send_dots)
    rcv_r[me] = snd_r[me // per_slab]
    ag_last(GRAD_OTHER)
    for c in crossing[GRAD_OWN]:
        c.wait_recv()
    g_grad, u_grad = whole(1), whole(2)
    in_rows = (dot(g_grad, gw[...], 1, 1) + dot(u_grad, uw[...], 1, 1)).astype(BF16)
    snd_i[...] = dot(grow, in_rows).reshape(n_expert, PAD, feat).astype(BF16)
    exchange(snd_i, rcv_i, 3)

    gg[...] = dot(xr[...], g_grad, 0, 0).astype(BF16)
    gu[...] = dot(xr[...], u_grad, 0, 0).astype(BF16)
    gd[...] = dot(hid, cr[...], 0, 0).astype(BF16)
    stores = []

    def store(src, dst):
        c = pltpu.make_async_copy(src, dst, out_sem.at[len(stores)])
        c.start()
        stores.append(c)

    store(gg, gg_hbm)
    store(gu, gu_hbm)
    store(gd, gd_hbm)
    for c in sent:
        c.wait_send()
    exchange_all(snd, rcv, 0).wait_send()

    exchange_all(snd_o, rcv_o, 2).wait_recv()
    back_out = rcv_o[...].reshape(padded, feat)
    mixed[...] = (p[0] * dot(take[0], back_out) + p[1] * dot(take[1], back_out)).astype(BF16)
    exchange_all(rcv_r, rcv_r, 1).wait_recv()
    dots = jnp.concatenate([rcv_r[j] for j in range(n_expert)], axis=0)
    high = dots.astype(BF16)
    rest = dots - high.astype(F32)
    middle = rest.astype(BF16)
    low = (rest - middle.astype(F32)).astype(BF16)
    lane = iota((toks, LANES), 1)
    start = (lax.rem(me, per_slab) * capacity).astype(F32)
    cols = []
    for k in range(2):
        from_expert = hot[k].astype(BF16)
        found = dot(from_expert, high) + dot(from_expert, middle) + dot(from_expert, low)
        picked = jnp.where(lane == start + pos_col[k], found, 0.0)
        cols.append(jnp.sum(picked, axis=1, keepdims=True) / p[k])
    groute[...] = jnp.concatenate(cols + [jnp.zeros((toks, toks - 2), F32)], axis=1).T[0:2, :]
    store(mixed, mixed_hbm)
    store(groute, groute_hbm)
    exchange_all(snd_i, rcv_i, 3).wait_recv()
    gtok[...] = dot(take[0] + take[1], rcv_i[...].reshape(padded, feat)).astype(BF16)
    store(gtok, gtok_hbm)
    exchange_all(snd_o, rcv_o, 2).wait_send()
    exchange_all(snd_i, rcv_i, 3).wait_send()
    exchange_all(rcv_r, rcv_r, 1).wait_send()
    for c in stores:
        c.wait()


def put_out(*refs):
    sem = refs[-1]
    n = (len(refs) - 1) // 3
    come = [pltpu.make_async_copy(refs[i], refs[2 * n + i], sem.at[0, i]) for i in range(n)]
    go = [pltpu.make_async_copy(refs[2 * n + i], refs[n + i], sem.at[1, i]) for i in range(n)]
    for c in come:
        c.start()
    for c, d in zip(come, go):
        c.wait()
        d.start()
    for d in go:
        d.wait()


def local(n_dp, n_expert, tokens, grad_out, expert_ids, route_weights, gate_weight, up_weight, down_weight):
    toks, feat = tokens.shape
    top = expert_ids.shape[1]
    hid = gate_weight.shape[2]
    nz = n_dp // 2
    capacity = max(2, 3 * toks * top // (2 * n_expert))
    rows = n_expert * capacity
    slab = rows // nz
    hop = max(1, nz // 2)
    hbm = pl.BlockSpec(memory_space=pltpu.HBM)
    wire = pltpu.VMEM((n_expert, PAD, feat), BF16)
    front = pltpu.VMEM((n_expert, 2 * feat // LANES * capacity // PAD, PAD, LANES), BF16)
    units = (9, slab, LANES)
    dma = pltpu.SemaphoreType.DMA
    shapes = (
        ((toks, feat), BF16),
        ((toks, feat), BF16),
        ((top, toks), F32),
        ((feat, hid), BF16),
        ((feat, hid), BF16),
        ((hid, feat), BF16),
    )
    out = pl.pallas_call(
        functools.partial(kernel, n_dp, n_expert, capacity),
        out_shape=tuple(jax.ShapeDtypeStruct(s, d) for s, d in shapes),
        in_specs=[hbm] * 7,
        out_specs=(hbm,) * 6,
        scratch_shapes=[
            pltpu.VMEM((toks, feat), BF16),
            pltpu.VMEM((toks, feat), BF16),
            pltpu.VMEM((top, toks), jnp.int32),
            pltpu.VMEM((top, toks), F32),
            pltpu.VMEM((feat, hid), BF16),
            pltpu.VMEM((feat, hid), BF16),
            pltpu.VMEM((hid, feat), BF16),
            *[front] * 2,
            *[wire] * 4,
            pltpu.VMEM((nz, 1, LANES), F32),
            pltpu.VMEM((n_expert, 1, LANES), F32),
            pltpu.VMEM((rows, feat), BF16),
            pltpu.VMEM((rows, feat), BF16),
            *[pltpu.VMEM(s, d) for s, d in shapes],
            pltpu.VMEM((2, nz, *units), BF16),
            pltpu.VMEM((2, 2, hop, *units), BF16),
            pltpu.VMEM((2, 2, hop, *units), BF16),
            pltpu.VMEM((nz, *units), BF16),
            pltpu.VMEM(units, BF16),
            pltpu.VMEM(units, BF16),
            pltpu.VMEM((2, nz, *units), BF16),
            pltpu.VMEM((2, nz, 8, LANES), F32),
            dma((7,)),
            dma((6,)),
            dma((8,)),
            dma((6, 2, hop)),
            dma((6, 2, hop)),
            dma((6, nz)),
            dma((6, nz)),
            dma((6,)),
            dma((6,)),
            dma((4, 2, hop)),
            dma((4, 2, hop)),
            dma((2, 2, hop + 1)),
            dma((2, 2, hop + 1)),
            dma((2, hop)),
            dma((2, hop)),
            dma((2, hop + 1)),
            dma((2, hop + 1)),
            dma((3,)),
            dma((3,)),
        ],
        compiler_params=pltpu.CompilerParams(
            collective_id=0, has_side_effects=True
        ),
        name="routed_layer",
    )(
        tokens, grad_out, expert_ids.T, route_weights.T,
        gate_weight.reshape(feat, hid), up_weight.reshape(feat, hid), down_weight.reshape(hid, feat),
    )
    mixed, gtok, groute, gg, gu, gd = pl.pallas_call(
        put_out,
        out_shape=tuple(jax.ShapeDtypeStruct(s, d) for s, d in shapes),
        in_specs=[hbm] * 6,
        out_specs=(hbm,) * 6,
        scratch_shapes=[pltpu.VMEM(s, d) for s, d in shapes] + [dma((2, 6))],
        name="put_out",
    )(*out)
    return mixed, gtok, groute.T, gg[None], gu[None], gd[None]


def solution(mesh):
    placed = (
        P("expert", "dp"),
        P("expert", "dp"),
        P("expert", None),
        P("expert", None),
        P("expert", "dp", None),
        P("expert", "dp", None),
        P("expert", None, "dp"),
    )
    return jax.shard_map(
        functools.partial(local, mesh.shape["dp"], mesh.shape["expert"]),
        mesh=mesh,
        in_specs=placed,
        out_specs=(
            P("expert", "dp"),
            P("expert", "dp"),
            P("expert", None),
            P("expert", "dp", None),
            P("expert", "dp", None),
            P("expert", None, "dp"),
        ),
        check_vma=False,
    )
```

time: 114 us -> 103 us (0.904)
  local copies, waits for them, and re-layouts: 8.65 us -> 0 us
  Pallas kernels: 104 us -> 102 us
    unnamed x22 -> x0, local copies, waits for them, and re-layouts: 8.65 us -> none
    pallas_call x1, Pallas kernels: 104 us -> 99.8 us  [local(): pl.pallas_call(functools.partial(kernel, n_dp, n_expert, capacity), out_s...]
    pallas_call x0 -> x1, Pallas kernels: none -> 2.19 us  [local(): pl.pallas_call(put_out, out_shape=tuple((jax.ShapeDtypeStruct(s, d) for s...]
where the time goes in v2:
time: 103 us
  Pallas kernels  102 us (99%)
    pallas_call x1, Pallas kernels, local(): pl.pallas_call(functools.partial(kernel, n_dp, n_expert, capacity), out_s...  99.8 us
    pallas_call x1, Pallas kernels, local(): pl.pallas_call(put_out, out_shape=tuple((jax.ShapeDtypeStruct(s, d) for s...  2.19 us

profile of v2, /device:TPU:1, one launch (start us, length us, event | category | flops | bytes accessed | tf_op | source)
XLA Modules:
  0.0 102.6 jit_solution(2706724117338116585)
XLA Ops:
  0.6 99.8 %routed_layer.1 = (bf16[128,256]{1,0:T(8,128)(2,1)}, bf16[128,256]{1,0:T(8,128)(2,1)}, f32[2,128]{1,0:T(2,128)}, bf16[256,768]{1,0:T(8,128)(2,1)}, bf16[256,768]{1,0:T(8,128)(2,1)}, /*index=5*/bf16[768,256]{1,0:T(8,128)(2,1)}) custom-call(bf16[128,256]{1,0:T(8,128)(2,1)} %tok_hbm.1, bf16[128,256]{1,0:T(8,128)(2,1)} %go_hbm.1, s32[2,128]{1,0:T(2,128)} %bitcast.12, ...), custom_call_target="tpu_custom_call" | custom-call | tf_op jit(solution)/shard_map/routed_layer/pallas_call | solution.py:502
  100.5 2.2 %put_out.1 = (bf16[128,256]{1,0:T(8,128)(2,1)}, bf16[128,256]{1,0:T(8,128)(2,1)}, f32[2,128]{1,0:T(2,128)}, bf16[256,768]{1,0:T(8,128)(2,1)}, bf16[256,768]{1,0:T(8,128)(2,1)}, /*index=5*/bf16[768,256]{1,0:T(8,128)(2,1)}) custom-call(bf16[128,256]{1,0:T(8,128)(2,1)} %get-tuple-element.18.refs_0_, bf16[128,256]{1,0:T(8,128)(2,1)} %get-tuple-element.19.refs_1_, ...), custom_call_target="tpu_custom_call" | custom-call | tf_op jit(solution)/shard_map/put_out/pallas_call | solution.py:558

commit v3 on v2

--- a/solution.py
+++ b/solution.py
@@ -22,8 +22,8 @@
     (True, 8, 1, True, 1),
 )
 HID_OWN, HID_OTHER, GRAD_OWN, GRAD_OTHER = range(4)
-GATHERS = ((True, 0, 3, 0), (False, 0, 2, 1), (True, 3, 6, 1), (False, 3, 3, 0))
-ACROSS = {HID_OWN: (2, 1), GRAD_OWN: (6, 3)}
+GATHERS = ((True, 0, 3, 0), (False, 0, 2, 1), (True, 3, 6, 1), (False, 3, 5, 0))
+ACROSS = {HID_OWN: (2, 1), GRAD_OWN: (8, 1)}
 
 
 def dot(a, b, ca=1, cb=0):
@@ -43,11 +43,11 @@
     tok_hbm, go_hbm, ids_hbm, rw_hbm, gw_hbm, uw_hbm, dw_hbm,
     mixed_hbm, gtok_hbm, groute_hbm, gg_hbm, gu_hbm, gd_hbm,
     tok, go, ids, rw, gw, uw, dw,
-    snd, rcv, snd_o, rcv_o, snd_i, rcv_i, snd_r, rcv_r, xr, cr,
+    snd, rcv, snd_o, rcv_o, snd_i, rcv_i, xr, cr,
     mixed, gtok, groute, gg, gu, gd,
     part, ring_in, ring_out, x_in, swap_out, swap_in, act, rd,
     in_sem, out_sem, a_sem, rs_send, rs_recv, x_send, x_recv, swap_send, swap_recv,
-    ag_send, ag_recv, cross_send, cross_recv, rd_send, rd_recv, rdx_send, rdx_recv, first_send, first_recv,
+    ag_send, ag_recv, cross_send, cross_recv, rd_send, rd_recv, first_send, first_recv,
 ):
     nz = n_dp // 2
     rows = n_expert * capacity
@@ -170,30 +170,44 @@
     earlier = one_hot(iota((toks, toks), 1) < iota((toks, toks), 0))
     before = dot(earlier, (hot[0] + hot[1]).astype(BF16))
     slot_cols = iota((toks, padded), 1)
-    take, pos_col = [], []
+    take, take_dot, pos_col = [], [], []
     for k in range(2):
         base = turned[:, k : k + 1] * PAD
         pos_col.append(jnp.sum(before * hot[k], axis=1, keepdims=True))
         take.append(one_hot(slot_cols == base + pos_col[k]))
+        take_dot.append(one_hot(slot_cols == base + capacity))
 
     g_col = iota((padded, 1), 0)
     g_group = jnp.floor((g_col + 0.5) / PAD)
     g_left = g_col - PAD * g_group
     g_row = jnp.where(g_left < capacity, capacity * g_group + g_left, -1.0)
     grow = one_hot(iota((padded, rows), 1) == g_row)
+    dot_row = jnp.where(g_left == capacity, jnp.floor((g_group + 0.5) / per_slab), -1.0)
+    place_dot = one_hot(iota((padded, 16), 1) == dot_row)
 
     long, short = nz // 2, nz // 2 - 1
     offsets = [long] + [sign * d for d in range(short, 0, -1) for sign in (1, -1)] + [0]
     sent = []
 
-    def go_on(src, dst, send_sem, recv_sem, who):
+    waits = {}
+
+    def go_on(src, dst, send_sem, recv_sem, who, once=None):
         c = pltpu.make_async_remote_copy(
             src_ref=src, dst_ref=dst, send_sem=send_sem, recv_sem=recv_sem,
             device_id=who, device_id_type=MESH,
         )
         c.start()
-        sent.append(c)
+        if once is None:
+            sent.append(c)
+        else:
+            waits[once[0]] = (once[1], send_sem)
         return c
+
+    def all_of(ref, send_sem, recv_sem):
+        return pltpu.make_async_remote_copy(
+            src_ref=ref, dst_ref=ref, send_sem=send_sem, recv_sem=recv_sem,
+            device_id=partner, device_id_type=MESH,
+        )
 
     def at_z(off):
         return lax.rem(z + nz + off, nz)
@@ -212,7 +226,8 @@
         for i, off in enumerate(offsets):
             x_late[k, off] = go_on(
                 part.at[half_of[False], at_z(off), pl.ds(u0, n)], x_in.at[at_z(off), pl.ds(u0, n)],
-                x_send.at[k, i], x_recv.at[k, i], partner,
+                x_send.at[int(k == UP_OWN)], x_recv.at[int(k == UP_OWN), i], partner,
+                ("x%d" % k, part.at[0, :, pl.ds(u0, n)]),
             )
 
     def mine(k, off):
@@ -242,7 +257,8 @@
                 ring_out[int(here), d, s, u0 : u0 + n] = value.astype(BF16)
                 src = ring_out.at[int(here), d, s, units]
             ring[k, d] = go_on(
-                src, ring_in.at[int(here), d, s, units], rs_send.at[k, d, s], rs_recv.at[k, d, s], toward[d]
+                src, ring_in.at[int(here), d, s, units], rs_send.at[k], rs_recv.at[k, d, s], toward[d],
+                ("s%d" % k, part.at[0, pl.ds(0, nz - 1), units]),
             )
 
     def total(k):
@@ -259,7 +275,7 @@
         _, u0, n, _, _ = SUMS[k]
         units = pl.ds(u0, n)
         swap_out[u0 : u0 + n] = total(k).astype(BF16)
-        return go_on(swap_out.at[units], swap_in.at[units], swap_send.at[k], swap_recv.at[k], partner)
+        return go_on(swap_out.at[units], swap_in.at[units], swap_send.at[int(k == BACK_OTHER)], swap_recv.at[int(k == BACK_OTHER)], partner)
 
     def swapped(k, c):
         _, u0, n, _, _ = SUMS[k]
@@ -319,10 +335,13 @@
         where = at_z(s if d else -s)
         h, units = half_of[here], pl.ds(u0, n)
         both = [
-            go_on(act.at[h, where, units], act.at[h, where, units], ag_send.at[k, d, s], ag_recv.at[k, d, s], toward[d])
+            go_on(
+                act.at[h, where, units], act.at[h, where, units], ag_send.at[k], ag_recv.at[k, d, s], toward[d],
+                ("g%d" % k, act.at[0, pl.ds(0, nz - 1), units]),
+            )
         ]
         if k == HID_OWN:
-            both.append(go_on(rd.at[h, where], rd.at[h, where], rd_send.at[d, s], rd_recv.at[d, s], toward[d]))
+            both.append(go_on(rd.at[h, where], rd.at[h, where], rd_send.at[0], rd_recv.at[d, s], toward[d], ("rd", rd.at[0, pl.ds(0, nz - 1)])))
         comes[k, d] = both
 
     def cross(k, s, d):
@@ -330,11 +349,16 @@
         u0, n = ACROSS[k]
         units = pl.ds(u0, n)
         j = int(k == GRAD_OWN)
-        crossing[k].append(
-            go_on(act.at[own, where, units], act.at[own, where, units], cross_send.at[j, d, s], cross_recv.at[j, d, s], partner)
+        some = act.at[0, pl.ds(0, nz - 1), units]
+        go_on(
+            act.at[own, where, units], act.at[own, where, units], cross_send.at[j], cross_recv.at[j], partner,
+            ("c%d" % k, some),
         )
+        crossing[k] = [(some, cross_send.at[j], cross_recv.at[j])]
         if k == HID_OWN:
-            crossing[k].append(go_on(rd.at[own, where], rd.at[own, where], rdx_send.at[d, s], rdx_recv.at[d, s], partner))
+            some = rd.at[0, pl.ds(0, nz - 1)]
+            go_on(rd.at[own, where], rd.at[own, where], cross_send.at[2], cross_recv.at[2], partner, ("cr", some))
+            crossing[k].append((some, cross_send.at[2], cross_recv.at[2]))
 
     def ag_step(k, s):
         here, _, _, far_way = GATHERS[k]
@@ -371,11 +395,12 @@
     first(HID_OWN, 0, 3)
     ag_step(HID_OWN, 0)
     first(GRAD_OWN, 3, 6)
+    ag_step(GRAD_OWN, 0)
     for job in (
-        (HID_OWN, 1), "hid", (HID_OTHER, 0), (GRAD_OWN, 0), "grad", (GRAD_OTHER, 0),
-        (HID_OWN, 2), (HID_OTHER, 1), (GRAD_OWN, 1), (GRAD_OTHER, 1),
-        (HID_OWN, 3), (HID_OTHER, 2), (GRAD_OWN, 2), (GRAD_OTHER, 2),
-        (HID_OWN, 4), (HID_OTHER, 3), (GRAD_OWN, 3), (GRAD_OTHER, 3), (GRAD_OWN, 4),
+        (HID_OWN, 1), "hid", (HID_OTHER, 0), (GRAD_OWN, 1), "grad", (GRAD_OTHER, 0),
+        (HID_OWN, 2), (HID_OTHER, 1), (GRAD_OWN, 2), (GRAD_OTHER, 1),
+        (HID_OWN, 3), (HID_OTHER, 2), (GRAD_OWN, 3), (GRAD_OTHER, 2),
+        (HID_OWN, 4), (HID_OTHER, 3), (GRAD_OWN, 4), (GRAD_OTHER, 3),
     ):
         if job in ("hid", "grad"):
             for c in firsts[HID_OWN if job == "hid" else GRAD_OWN]:
@@ -384,7 +409,7 @@
             ag_step(*job)
     ag_last(HID_OTHER)
     for c in crossing[HID_OWN]:
-        c.wait_recv()
+        all_of(*c).wait_recv()
 
     def whole(a):
         return jnp.concatenate(
@@ -393,24 +418,22 @@
 
     hid = whole(0)
     out_rows = dot(hid, dw[...]).astype(BF16)
-    for j in range(nz):
-        snd_r[j] = rd[0, j, 0:1, :] + rd[1, j, 0:1, :]
+    dots = jnp.concatenate([rd[0, j, 0:1, :] + rd[1, j, 0:1, :] for j in range(nz)], axis=0)
+    dots = jnp.concatenate([dots, jnp.zeros((16 - nz, LANES), F32)], axis=0)
+    high = dots.astype(BF16)
+    low = (dots - high.astype(F32)).astype(BF16)
     spread = dot(grow, out_rows)
+    spread = jnp.concatenate(
+        [spread[:, :LANES] + dot(place_dot, high), spread[:, LANES : 2 * LANES] + dot(place_dot, low)]
+        + ([spread[:, 2 * LANES :]] if feat > 2 * LANES else []),
+        axis=1,
+    )
     snd_o[...] = spread.reshape(n_expert, PAD, feat).astype(BF16)
     exchange(snd_o, rcv_o, 2)
 
-    def send_dots(to):
-        pltpu.make_async_remote_copy(
-            src_ref=snd_r.at[to // per_slab], dst_ref=rcv_r.at[me],
-            send_sem=a_sem.at[2], recv_sem=a_sem.at[3],
-            device_id=(me_dp, to), device_id_type=MESH,
-        ).start()
-
-    each_peer(send_dots)
-    rcv_r[me] = snd_r[me // per_slab]
     ag_last(GRAD_OTHER)
     for c in crossing[GRAD_OWN]:
-        c.wait_recv()
+        all_of(*c).wait_recv()
     g_grad, u_grad = whole(1), whole(2)
     in_rows = (dot(g_grad, gw[...], 1, 1) + dot(u_grad, uw[...], 1, 1)).astype(BF16)
     snd_i[...] = dot(grow, in_rows).reshape(n_expert, PAD, feat).astype(BF16)
@@ -431,24 +454,19 @@
     store(gd, gd_hbm)
     for c in sent:
         c.wait_send()
+    for ref, sem in waits.values():
+        all_of(ref, sem, first_recv.at[0]).wait_send()
     exchange_all(snd, rcv, 0).wait_send()
 
     exchange_all(snd_o, rcv_o, 2).wait_recv()
     back_out = rcv_o[...].reshape(padded, feat)
     mixed[...] = (p[0] * dot(take[0], back_out) + p[1] * dot(take[1], back_out)).astype(BF16)
-    exchange_all(rcv_r, rcv_r, 1).wait_recv()
-    dots = jnp.concatenate([rcv_r[j] for j in range(n_expert)], axis=0)
-    high = dots.astype(BF16)
-    rest = dots - high.astype(F32)
-    middle = rest.astype(BF16)
-    low = (rest - middle.astype(F32)).astype(BF16)
     lane = iota((toks, LANES), 1)
     start = (lax.rem(me, per_slab) * capacity).astype(F32)
     cols = []
     for k in range(2):
-        from_expert = hot[k].astype(BF16)
-        found = dot(from_expert, high) + dot(from_expert, middle) + dot(from_expert, low)
-        picked = jnp.where(lane == start + pos_col[k], found, 0.0)
+        found = dot(take_dot[k], back_out)
+        picked = jnp.where(lane == start + pos_col[k], found[:, :LANES] + found[:, LANES : 2 * LANES], 0.0)
         cols.append(jnp.sum(picked, axis=1, keepdims=True) / p[k])
     groute[...] = jnp.concatenate(cols + [jnp.zeros((toks, toks - 2), F32)], axis=1).T[0:2, :]
     store(mixed, mixed_hbm)
@@ -458,7 +476,6 @@
     store(gtok, gtok_hbm)
     exchange_all(snd_o, rcv_o, 2).wait_send()
     exchange_all(snd_i, rcv_i, 3).wait_send()
-    exchange_all(rcv_r, rcv_r, 1).wait_send()
     for c in stores:
         c.wait()
 
@@ -514,8 +531,6 @@
             pltpu.VMEM((hid, feat), BF16),
             *[front] * 2,
             *[wire] * 4,
-            pltpu.VMEM((nz, 1, LANES), F32),
-            pltpu.VMEM((n_expert, 1, LANES), F32),
             pltpu.VMEM((rows, feat), BF16),
             pltpu.VMEM((rows, feat), BF16),
             *[pltpu.VMEM(s, d) for s, d in shapes],
@@ -530,20 +545,18 @@
             dma((7,)),
             dma((6,)),
             dma((8,)),
+            dma((6,)),
             dma((6, 2, hop)),
-            dma((6, 2, hop)),
-            dma((6, nz)),
-            dma((6, nz)),
-            dma((6,)),
-            dma((6,)),
+            dma((2,)),
+            dma((2, nz)),
+            dma((2,)),
+            dma((2,)),
+            dma((4,)),
             dma((4, 2, hop)),
-            dma((4, 2, hop)),
-            dma((2, 2, hop + 1)),
-            dma((2, 2, hop + 1)),
+            dma((3,)),
+            dma((3,)),
+            dma((1,)),
             dma((2, hop)),
-            dma((2, hop)),
-            dma((2, hop + 1)),
-            dma((2, hop + 1)),
             dma((3,)),
             dma((3,)),
         ],

time: 103 us -> 98.2 us (0.953)
  Pallas kernels: 102 us -> 97.4 us
    pallas_call x1, Pallas kernels: 99.8 us -> 95.2 us  [local(): pl.pallas_call(functools.partial(kernel, n_dp, n_expert, capacity), out_s...]
where the time goes in v3:
time: 98.2 us; the launch traced here: 98 us
  Pallas kernels  97.4 us (99%)
    pallas_call x1, Pallas kernels, local(): pl.pallas_call(functools.partial(kernel, n_dp, n_expert, capacity), out_s...  95.2 us
    pallas_call x1, Pallas kernels, local(): pl.pallas_call(put_out, out_shape=tuple((jax.ShapeDtypeStruct(s, d) for s...  2.19 us

profile of v3, /device:TPU:1, one launch (start us, length us, event | category | flops | bytes accessed | tf_op | source)
XLA Modules:
  0.0 98.0 jit_solution(12322807742112887061)
XLA Ops:
  0.6 95.2 %routed_layer.1 = (bf16[128,256]{1,0:T(8,128)(2,1)}, bf16[128,256]{1,0:T(8,128)(2,1)}, f32[2,128]{1,0:T(2,128)}, bf16[256,768]{1,0:T(8,128)(2,1)}, bf16[256,768]{1,0:T(8,128)(2,1)}, /*index=5*/bf16[768,256]{1,0:T(8,128)(2,1)}) custom-call(bf16[128,256]{1,0:T(8,128)(2,1)} %tok_hbm.1, bf16[128,256]{1,0:T(8,128)(2,1)} %go_hbm.1, s32[2,128]{1,0:T(2,128)} %bitcast.12, ...), custom_call_target="tpu_custom_call" | custom-call | tf_op jit(solution)/shard_map/routed_layer/pallas_call | solution.py:519
  95.8 2.2 %put_out.1 = (bf16[128,256]{1,0:T(8,128)(2,1)}, bf16[128,256]{1,0:T(8,128)(2,1)}, f32[2,128]{1,0:T(2,128)}, bf16[256,768]{1,0:T(8,128)(2,1)}, bf16[256,768]{1,0:T(8,128)(2,1)}, /*index=5*/bf16[768,256]{1,0:T(8,128)(2,1)}) custom-call(bf16[128,256]{1,0:T(8,128)(2,1)} %get-tuple-element.18.refs_0_, bf16[128,256]{1,0:T(8,128)(2,1)} %get-tuple-element.19.refs_1_, ...), custom_call_target="tpu_custom_call" | custom-call | tf_op jit(solution)/shard_map/put_out/pallas_call | solution.py:571
